TPU v7x, 8 devices: a whole 2x2x1 slice. The times are simulated.
8 devices in a mesh: data: 1 (over z), pipe: 8 (over y, x, core).
Axes of the slice: x: 2, y: 2, z: 1, core: 2. Of those that a mesh axis runs over, the one named last changes fastest.
Arguments:
- x_slice: bfloat16 [2048, 2048], P(('data', 'pipe'))
- slice_idx: int32 [8], P(('data', 'pipe'))
- k_cache: bfloat16 [30720, 24, 128], P(('data', 'pipe'))
- v_cache: bfloat16 [30720, 24, 128], P(('data', 'pipe'))
- w_q: bfloat16 [8, 2048, 3072], P('pipe')
- w_kv: bfloat16 [8, 2048, 6144], P('pipe')
- w_o: bfloat16 [8, 3072, 2048], P('pipe')
- w_gate: bfloat16 [8, 2048, 8192], P('pipe')
- w_up: bfloat16 [8, 2048, 8192], P('pipe')
- w_down: bfloat16 [8, 8192, 2048], P('pipe')
Outputs:
- output 1: bfloat16 [2048, 2048], P(('data', 'pipe'))
- output 2: float32 [2048, 24], P(('data', 'pipe'))
All inputs are finite; a program needn't handle non-finite values.
Results may differ from a plain program's by a relative error of at most 0.00906081.
Values are sent between devices in bfloat16 or wider.
A program may use at most 1 GiB of HBM per device.

v0:
```python
import math

import jax
import jax.numpy as jnp
from jax import lax
from jax.experimental import pallas as pl
from jax.experimental.pallas import tpu as pltpu
from jax.sharding import PartitionSpec as P

BF = jnp.bfloat16
F32 = jnp.float32
HD = 128
TN = 512
TK = 2048
RING = 12
AHEAD = 4
KRAW = 3
VRAW = 4
KB = 256
FLOOR = -1e30
LIMIT = 2.0 ** 15
HBM = pl.BlockSpec(memory_space=pltpu.HBM)
SM = pl.BlockSpec(memory_space=pltpu.SMEM)


def rms(values):
    v = values.astype(F32)
    return (v * lax.rsqrt(jnp.mean(v * v, axis=-1, keepdims=True) + 1e-6)).astype(BF)


def dot(a, b):
    return jnp.dot(a, b, preferred_element_type=F32)


def layer_kernel(idx_ref, x_hbm, k_hbm, v_hbm, wq, wkv, wo, wg, wu, t_hbm, h_hbm, lse_hbm,
                 ring, kraw, vraw, kt, kn, vn, qa, acc, pa, pb, mu_s, l_s, lb_s,
                 x_s, a_s, o_s, h_s, t_s, lse_s, wsem, ksem, msem, tsem):
    n = idx_ref[0]
    rows, dm = x_s.shape
    heads = qa.shape[0]
    c = HD ** -0.5 * math.log2(math.e)
    log2 = math.log(2.0)

    def col(i, w=TN):
        return pl.ds(pl.multiple_of(i * w, w), w)

    def fetch(e, src, height=TK):
        s = lax.rem(e, RING)
        pltpu.make_async_copy(src, ring.at[s, pl.ds(0, height)], wsem.at[s]).start()

    def ready(e, height=TK):
        s = lax.rem(e, RING)
        pltpu.make_async_copy(wg.at[pl.ds(0, height), pl.ds(0, TN)], ring.at[s, pl.ds(0, height)], wsem.at[s]).wait()
        return s

    def fetch_wo(e, nt):
        fetch(e, wo.at[pl.ds(0, TK), col(nt)])
        fetch(e + 1, wo.at[pl.ds(TK, wo.shape[0] - TK), col(nt)], wo.shape[0] - TK)

    def fetch_gu(e, nt):
        fetch(e, wg.at[:, col(nt)])
        fetch(e + 1, wu.at[:, col(nt)])

    def fetch_mid(e):
        rest = wo.shape[0] - TK
        even = lax.rem(e, 2) == 0
        nt = lax.div(e - 18, 2)

        @pl.when(jnp.logical_and(e < 26, even))
        def _():
            fetch(e, wo.at[pl.ds(0, TK), col(nt)])

        @pl.when(jnp.logical_and(e < 26, jnp.logical_not(even)))
        def _():
            fetch(e, wo.at[pl.ds(TK, rest), col(nt)], rest)

        @pl.when(jnp.logical_and(e >= 26, even))
        def _():
            fetch(e, wg.at[:, col(nt - 4)])

        @pl.when(jnp.logical_and(e >= 26, jnp.logical_not(even)))
        def _():
            fetch(e, wu.at[:, col(nt - 4)])

    xcopy = pltpu.make_async_copy(x_hbm, x_s, msem.at[0])
    xcopy.start()
    for e in range(AHEAD):
        fetch(e, wq.at[:, pl.ds(e * TN, TN)])

    def kv_copies(b):
        s, t = lax.rem(b, KRAW), lax.rem(b, VRAW)
        return [
            pltpu.make_async_copy(k_hbm.at[pl.ds(b * KB, KB)], kraw.at[s], ksem.at[0, s]),
            pltpu.make_async_copy(v_hbm.at[pl.ds(b * KB, KB)], vraw.at[t], ksem.at[1, t]),
        ]

    def kv_start(b):
        @pl.when(b < n)
        def _():
            for d in kv_copies(b):
                d.start()

    qa[:, HD:] = jnp.zeros((heads, qa.shape[1] - HD, rows), BF)
    xcopy.wait()
    a_s[...] = rms(x_s[...])

    def q_step(i, _):
        @pl.when(i == 0)
        def _():
            for d in range(AHEAD, 6):
                fetch(d, wq.at[:, pl.ds(d * TN, TN)])

        @pl.when(i > 0)
        def _():
            for d in range(2):
                fetch(2 * i + AHEAD + d, wkv.at[:, col(2 * i + AHEAD + d - 6)])

        for d in range(2):
            e = 2 * i + d
            s = ready(e)
            t = dot(a_s[...], ring[s]).astype(BF)
            for j in range(4):
                qa[4 * e + j, 0:HD] = t[:, j * HD:(j + 1) * HD].T
        return 0

    lax.fori_loop(0, 3, q_step, 0)

    def fetch_kv(e):
        for d in range(2):
            fetch(e + d, wkv.at[:, col(e + d - 6)])

    def kv_tiles(e, dst, base):
        for d in range(2):
            s = ready(e + d)
            t = dot(a_s[...], ring[s]).astype(BF)
            for j in range(4):
                dst[base + 4 * d + j] = t[:, j * HD:(j + 1) * HD]

    def k_step(i, _):
        e = 6 + 2 * i
        fetch_kv(e + AHEAD)
        kv_tiles(e, kn, 8 * i)
        return 0

    lax.fori_loop(0, 3, k_step, 0)
    fetch_kv(12 + AHEAD)
    kv_start(0)
    kv_start(1)
    kv_tiles(12, vn, 0)

    def v_step(i, _):
        e = 14 + 2 * i
        fetch_wo(e + AHEAD, i)
        kv_tiles(e, vn, 8 * i + 8)
        return 0

    lax.fori_loop(0, 2, v_step, 0)

    def bf_round(v):
        return v.astype(BF).astype(F32)

    def set_shift(h, mu):
        mu_s[h] = mu
        first = lax.broadcasted_iota(jnp.int32, (16, rows), 0) == 0
        qa[h, HD:HD + 16] = jnp.where(first, -mu, 0.0).astype(BF)

    vis = lax.broadcasted_iota(jnp.int32, (KB, rows), 0) <= lax.broadcasted_iota(jnp.int32, (KB, rows), 1)

    def local(h, _):
        s = jnp.where(vis, dot(kn[h], qa[h, 0:HD]), FLOOR)
        mu = bf_round(jnp.max(s, axis=0, keepdims=True))
        e = jnp.exp2((s - mu) * c)
        l_s[h] = jnp.sum(e, axis=0, keepdims=True)
        acc[h] = dot(vn[h].T, e.astype(BF))
        set_shift(h, mu)
        return 0

    @pl.when(n == 0)
    def _():
        lax.fori_loop(0, heads, local, 0, unroll=4)

    def exact(h, cur):
        s = dot(kt[h], qa[h, 0:HD])
        mo = mu_s[h]
        mu = jnp.maximum(mo, bf_round(jnp.max(s, axis=0, keepdims=True)))
        al = jnp.exp2((mo - mu) * c)
        e = jnp.exp2((s - mu) * c)
        l_s[h] = l_s[h] * al
        acc[h] = acc[h] * al
        lb_s[h] = jnp.sum(e, axis=0, keepdims=True)
        cur[h] = e.astype(BF)
        set_shift(h, mu)

    def exact_all(b, cur):
        kt[...] = jnp.swapaxes(kraw[lax.rem(b, KRAW)], 0, 1)

        def one(h, _):
            exact(h, cur)
            return 0
        lax.fori_loop(0, heads, one, 0, unroll=2)

    ones = jnp.where(lax.broadcasted_iota(jnp.int32, (KB, HD), 1) == 0, 1.0, 0.0).astype(BF)
    k2 = kraw.reshape(KRAW, KB * heads, HD)
    v2 = vraw.reshape(VRAW, KB * heads, HD)

    def fast(h, cur, slot):
        k = k2.at[slot][pl.ds(h, KB, stride=heads), :]
        e = jnp.exp2(dot(jnp.concatenate([k, ones], axis=1), qa[h]) * c)
        cur[h] = e.astype(BF)
        lb_s[h] = jnp.sum(e, axis=0, keepdims=True)

    def value(h, prev, slot):
        v = v2.at[slot][pl.ds(h, KB, stride=heads), :]
        l_s[h] = l_s[h] + lb_s[h]
        acc[h] = acc[h] + dot(v.T, prev[h])

    def first(h):
        q = qa[h, 0:HD]
        s0 = jnp.where(vis, dot(kn[h], q), FLOOR)
        s1 = dot(k2.at[0][pl.ds(h, KB, stride=heads), :], q)
        mu = bf_round(jnp.maximum(jnp.max(s0, axis=0, keepdims=True), jnp.max(s1, axis=0, keepdims=True)))
        e0 = jnp.exp2((s0 - mu) * c)
        e1 = jnp.exp2((s1 - mu) * c)
        l_s[h] = jnp.sum(e0, axis=0, keepdims=True)
        lb_s[h] = jnp.sum(e1, axis=0, keepdims=True)
        pa[h] = e1.astype(BF)
        acc[h] = dot(vn[h].T, e0.astype(BF))
        set_shift(h, mu)

    @pl.when(n > 0)
    def _():
        for d in kv_copies(0):
            d.wait()
        kv_start(2)
        for h in range(heads):
            first(h)

        def block(b, prev, cur):
            for d in kv_copies(b):
                d.wait()
            kv_start(b + 2)

            @pl.when(b <= 8)
            def _():
                fetch_mid(21 + b)

            ks, vs = lax.rem(b, KRAW), lax.rem(b - 1, VRAW)
            for h in range(heads):
                value(h, prev, vs)
                fast(h, cur, ks)

            @pl.when(jnp.logical_not(jnp.max(lb_s[...]) <= LIMIT))
            def _():
                exact_all(b, cur)

        def two(i, _):
            b = 2 * i + 1
            block(b, pa, pb)

            @pl.when(b + 1 < n)
            def _():
                block(b + 1, pb, pa)

            return 0

        lax.fori_loop(0, lax.div(n, 2), two, 0)

        @pl.when(lax.rem(n, 2) == 1)
        def _():
            for h in range(heads):
                value(h, pa, lax.rem(n - 1, VRAW))

        @pl.when(lax.rem(n, 2) == 0)
        def _():
            for h in range(heads):
                value(h, pb, lax.rem(n - 1, VRAW))

    def late(e, _):
        fetch_mid(e)
        return 0

    lax.fori_loop(22 + jnp.clip(n - 1, 0, 8), 30, late, 0)
    for h in range(heads):
        l = l_s[h]
        o_s[:, h * HD:(h + 1) * HD] = (acc[h] * (1.0 / l)).T.astype(BF)
        lse_s[pl.ds(h, 1)] = mu_s[h] * (HD ** -0.5) + jnp.log2(l) * log2
    lcopy = pltpu.make_async_copy(lse_s, lse_hbm, msem.at[1])
    lcopy.start()

    def o_step(i, _):
        rest = wo.shape[0] - TK
        slots = [(ready(18 + 4 * i + 2 * d), ready(19 + 4 * i + 2 * d, rest)) for d in range(2)]
        for d in range(2):
            s0, s1 = slots[d]
            cols = col(2 * i + d)
            r = dot(o_s[:, 0:TK], ring[s0]) + dot(o_s[:, TK:], ring[s1, pl.ds(0, rest)])
            h_s[:, cols] = (x_s[:, cols].astype(F32) + r).astype(BF)
        for d in range(2):
            fetch_gu(18 + 4 * i + 2 * d + RING, 2 * i + d + 2)
        return 0

    lax.fori_loop(0, 2, o_step, 0)
    a_s[...] = rms(h_s[...])

    hcopy = pltpu.make_async_copy(h_s, h_hbm, msem.at[2])
    hcopy.start()

    def t_copy(nt):
        return pltpu.make_async_copy(t_s.at[:, col(nt)], t_hbm.at[:, col(nt)], tsem.at[nt])

    def gu_pair(p):
        e = 26 + 4 * p
        slots = [ready(e + d) for d in range(4)]
        for d in range(2):
            g = dot(a_s[...], ring[slots[2 * d]])
            u = dot(a_s[...], ring[slots[2 * d + 1]])
            t_s[:, col(2 * p + d)] = (jax.nn.silu(g) * u).astype(BF)
        for d in range(2):
            t_copy(2 * p + d).start()

    def gu1(p, _):
        gu_pair(p)
        for d in range(2):
            fetch_gu(26 + 4 * p + 2 * d + RING, 2 * p + d + 6)
        return 0

    def gu2(p, _):
        gu_pair(p)
        return 0

    def drain(nt, _):
        t_copy(nt).wait()
        return 0

    lax.fori_loop(0, 5, gu1, 0)
    lax.fori_loop(5, 8, gu2, 0)
    lcopy.wait()
    hcopy.wait()
    lax.fori_loop(0, 16, drain, 0)


def down_kernel(stages, t_hbm, h_hbm, wd, y_hbm, w_s, t_s, h_s, y_s, r_s, wsem, tsem, hsem, send, recv):
    me = lax.axis_index('pipe')
    nxt = lax.rem(me + 1, stages)
    prev = lax.rem(me + stages - 1, stages)
    chunks = w_s.shape[0]
    parts = t_s.shape[0]
    width = w_s.shape[2]
    depth = t_s.shape[2]
    barrier = pltpu.get_barrier_semaphore()
    pl.semaphore_signal(barrier, inc=1, device_id={'pipe': prev}, device_id_type=pl.DeviceIdType.MESH)

    def wcopy(i, k):
        return pltpu.make_async_copy(
            wd.at[pl.ds(k * depth, depth), pl.ds(i * width, width)], w_s.at[i, pl.ds(k * depth, depth)], wsem.at[i, k])

    tcopies = [pltpu.make_async_copy(t_hbm.at[:, pl.ds(k * depth, depth)], t_s.at[k], tsem.at[k]) for k in range(parts)]
    hcopy = pltpu.make_async_copy(h_hbm, h_s, hsem)
    pieces = [(i, k) for i in range(chunks) for k in range(parts)]
    ahead = 4
    for p in range(ahead):
        if p < parts:
            tcopies[p].start()
        wcopy(*pieces[p]).start()
    hcopy.start()

    def out(i):
        cols = pl.ds(i * width, width)
        return pltpu.make_async_remote_copy(
            src_ref=y_s.at[:, cols], dst_ref=y_hbm.at[:, cols], send_sem=send.at[i], recv_sem=recv.at[i],
            device_id={'pipe': nxt}, device_id_type=pl.DeviceIdType.MESH)

    for i in range(chunks):
        cols = pl.ds(i * width, width)
        for k in range(parts):
            p = i * parts + k
            if i == 0:
                tcopies[k].wait()
            wcopy(i, k).wait()
            if p + ahead < len(pieces):
                wcopy(*pieces[p + ahead]).start()
            d = dot(t_s[k], w_s[i, pl.ds(k * depth, depth)])
            r_s[...] = d if k == 0 else r_s[...] + d
        if i == 0:
            hcopy.wait()
        y_s[:, cols] = (h_s[:, cols].astype(F32) + r_s[...]).astype(BF)
        if i == 0:
            pl.semaphore_wait(barrier, 1)
        out(i).start()
    for i in range(chunks):
        out(i).wait()


def down_call(t, h, wd, stages, width=512, parts=4):
    rows, dm = h.shape
    ff = t.shape[1]
    chunks = dm // width
    vm = pltpu.VMEM
    return pl.pallas_call(
        lambda *r: down_kernel(stages, *r),
        in_specs=[HBM] * 3,
        out_specs=pl.BlockSpec(memory_space=pltpu.VMEM),
        out_shape=jax.ShapeDtypeStruct((rows, dm), BF),
        scratch_shapes=[
            vm((chunks, ff, width), BF),
            vm((parts, rows, ff // parts), BF),
            vm((rows, dm), BF),
            vm((rows, dm), BF),
            vm((rows, width), F32),
            pltpu.SemaphoreType.DMA((chunks, parts)),
            pltpu.SemaphoreType.DMA((parts,)),
            pltpu.SemaphoreType.DMA,
            pltpu.SemaphoreType.DMA((chunks,)),
            pltpu.SemaphoreType.DMA((chunks,)),
        ],
        compiler_params=pltpu.CompilerParams(vmem_limit_bytes=48 * 2**20, collective_id=0, has_side_effects=True),
    )(t, h, wd)


def layer_call(idx, x, k, v, wq, wkv, wo, wg, wu, wd=None):
    rows, dm = x.shape
    ff = wg.shape[1]
    heads, hd = k.shape[1:]
    vm = pltpu.VMEM
    return pl.pallas_call(
        layer_kernel,
        in_specs=[SM] + [HBM] * 8,
        out_specs=[HBM] * 3,
        out_shape=[jax.ShapeDtypeStruct((rows, ff), BF), jax.ShapeDtypeStruct((rows, dm), BF), jax.ShapeDtypeStruct((heads, rows), F32)],
        scratch_shapes=[
            vm((RING, TK, TN), BF),
            vm((KRAW, KB, heads, hd), BF),
            vm((VRAW, KB, heads, hd), BF),
            vm((heads, KB, hd), BF),
            vm((heads, rows, hd), BF),
            vm((heads, rows, hd), BF),
            vm((heads, 2 * hd, rows), BF),
            vm((heads, hd, rows), F32),
            vm((heads, KB, rows), BF),
            vm((heads, KB, rows), BF),
            vm((heads, 1, rows), F32),
            vm((heads, 1, rows), F32),
            vm((heads, 1, rows), F32),
            vm((rows, dm), BF),
            vm((rows, dm), BF),
            vm((rows, heads * hd), BF),
            vm((rows, dm), BF),
            vm((rows, ff), BF),
            vm((heads, rows), F32),
            pltpu.SemaphoreType.DMA((RING,)),
            pltpu.SemaphoreType.DMA((2, VRAW)),
            pltpu.SemaphoreType.DMA((3,)),
            pltpu.SemaphoreType.DMA((16,)),
        ],
        compiler_params=pltpu.CompilerParams(vmem_limit_bytes=67043328),
    )(idx, x, k, v, wq, wkv, wo, wg, wu)


def solution(mesh):
    stages = mesh.shape['pipe']

    def device_step(x, idx, k, v, w_q, w_kv, w_o, w_gate, w_up, w_down):
        t, h, lse = layer_call(idx, x, k, v, w_q[0], w_kv[0], w_o[0], w_gate[0], w_up[0])
        return down_call(t, h, w_down[0], stages), lse.T

    rows_spec = P(('data', 'pipe'), None)
    cache_spec = P(('data', 'pipe'), None, None)
    stage_spec = P('pipe', None, None)
    return jax.shard_map(
        device_step,
        mesh=mesh,
        in_specs=(rows_spec, P(('data', 'pipe')), cache_spec, cache_spec) + (stage_spec,) * 6,
        out_specs=(rows_spec, rows_spec),
        check_vma=False,
    )
```

profile of v0, /device:TPU:0, one launch (start us, length us, event | category | flops | bytes accessed | tf_op | source)
XLA Modules:
  0.0 95.9 jit_solution(8634426031765737998)
XLA Ops:
  1.3 55.7 %shard_map.113 = (bf16[256,8192]{1,0:T(8,128)(2,1)}, bf16[256,2048]{1,0:T(8,128)(2,1)}, f32[24,256]{1,0:T(8,128)}) custom-call(s32[1]{0:T(128)S(6)} %copy.13.idx_ref, bf16[256,2048]{1,0:T(8,128)(2,1)} %x_hbm.1, bf16[3840,24,128]{2,1,0:T(8,128)(2,1)} %k_hbm.1, bf16[3840,24,128]{2,1,0:T(8,128)(2,1)} %v_hbm.1, bf16[2048,3072]{1,0:T(8,128)(2,1)} %bitcast.11, ...), custom_call_target="tpu_custom_call" | custom-call | tf_op jit(solution)/shard_map/pallas_call | solution.py:425
  56.9 0.0 copy-start
  57.0 1.2 %copy-done = bf16[256,2048]{1,0:T(8,128)(2,1)S(1)} copy-done((bf16[256,2048]{1,0:T(8,128)(2,1)S(1)}, bf16[256,2048]{1,0:T(8,128)(2,1)}, u32[]{:S(2)}) %copy-start) | copy-done | bytes 1048600
  58.2 36.7 %shard_map.114 = bf16[256,2048]{1,0:T(8,128)(2,1)S(1)} custom-call(bf16[256,8192]{1,0:T(8,128)(2,1)} %get-tuple-element.5.r_0_, bf16[256,2048]{1,0:T(8,128)(2,1)S(1)} %copy-done, bf16[8192,2048]{1,0:T(8,128)(2,1)} %bitcast.9), custom_call_target="tpu_custom_call" | custom-call | tf_op jit(solution)/shard_map/pallas_call | solution.py:399
  94.9 1.0 %copy.14 = bf16[256,2048]{1,0:T(8,128)(2,1)} copy(bf16[256,2048]{1,0:T(8,128)(2,1)S(1)} %shard_map.114) | data formatting | bytes 2097152
Async XLA Ops:
  56.9 1.2 %copy-start = (bf16[256,2048]{1,0:T(8,128)(2,1)S(1)}, bf16[256,2048]{1,0:T(8,128)(2,1)}, u32[]{:S(2)}) copy-start(bf16[256,2048]{1,0:T(8,128)(2,1)} %get-tuple-element.6.r_1_) | copy-start | bytes 3145732
where the time goes:
time: 96.5 us; the launch traced here: 95.9 us
  Pallas kernels  92.4 us (96%)
  local copies, waits for them, and re-layouts  2.19 us (2%)
  between operations  1.3 us (1%)
    pallas_call x1, Pallas kernels, layer_call(): pl.pallas_call(layer_kernel, in_specs=[SM] + [HBM] * 8, out_specs=[HBM] *...  55.7 us
    pallas_call x1, Pallas kernels, down_call(): pl.pallas_call(lambda *r: down_kernel(stages, *r), in_specs=[HBM] * 3, ou...  36.7 us
    unnamed x3, local copies, waits for them, and re-layouts  2.19 us

commit v1 on v0

--- a/solution.py
+++ b/solution.py
@@ -414,7 +414,7 @@
             pltpu.SemaphoreType.DMA((chunks,)),
         ],
         compiler_params=pltpu.CompilerParams(vmem_limit_bytes=48 * 2**20, collective_id=0, has_side_effects=True),
-    )(t, h, wd)
+    )(t, pltpu.with_memory_space_constraint(h, pltpu.HBM), wd)
 
 
 def layer_call(idx, x, k, v, wq, wkv, wo, wg, wu, wd=None):

time: 96.5 us -> 98.2 us (1.018); the launches traced: 95.9 us -> 99.5 us
  Pallas kernels: 92.4 us -> 95 us
    pallas_call x1, Pallas kernels: 55.7 us -> 58.4 us  [layer_call(): pl.pallas_call(layer_kernel, in_specs=[SM] + [HBM] * 8, out_specs=[HBM] *...]
where the time goes in v1:
time: 98.2 us; the launch traced here: 99.5 us
  Pallas kernels  95 us (97%)
  local copies, waits for them, and re-layouts  3.15 us (3%)
  between operations  1.3 us (1%)
    pallas_call x1, Pallas kernels, layer_call(): pl.pallas_call(layer_kernel, in_specs=[SM] + [HBM] * 8, out_specs=[HBM] *...  58.4 us
    pallas_call x1, Pallas kernels, down_call(): pl.pallas_call(lambda *r: down_kernel(stages, *r), in_specs=[HBM] * 3, ou...  36.7 us
    unnamed x3, local copies, waits for them, and re-layouts  3.15 us

profile of v1, /device:TPU:0, one launch (start us, length us, event | category | flops | bytes accessed | tf_op | source)
XLA Modules:
  0.0 99.5 jit_solution(3814808938707208104)
XLA Ops:
  1.3 58.4 %shard_map.113 = (bf16[256,8192]{1,0:T(8,128)(2,1)}, bf16[256,2048]{1,0:T(8,128)(2,1)}, f32[24,256]{1,0:T(8,128)}) custom-call(s32[1]{0:T(128)S(6)} %copy.13.idx_ref, bf16[256,2048]{1,0:T(8,128)(2,1)} %x_hbm.1, bf16[3840,24,128]{2,1,0:T(8,128)(2,1)} %k_hbm.1, bf16[3840,24,128]{2,1,0:T(8,128)(2,1)} %v_hbm.1, bf16[2048,3072]{1,0:T(8,128)(2,1)} %bitcast.11, ...), custom_call_target="tpu_custom_call" | custom-call | tf_op jit(solution)/shard_map/pallas_call | solution.py:425
  59.7 0.0 copy-start
  59.7 2.2 %copy-done = bf16[256,8192]{1,0:T(8,128)(2,1)S(1)} copy-done((bf16[256,8192]{1,0:T(8,128)(2,1)S(1)}, bf16[256,8192]{1,0:T(8,128)(2,1)}, u32[]{:S(2)}) %copy-start) | copy-done | bytes 4194328
  61.8 36.7 %shard_map.114 = bf16[256,2048]{1,0:T(8,128)(2,1)S(1)} custom-call(bf16[256,8192]{1,0:T(8,128)(2,1)S(1)} %copy-done, bf16[256,2048]{1,0:T(8,128)(2,1)} %get-tuple-element.6.r_1_, bf16[8192,2048]{1,0:T(8,128)(2,1)} %bitcast.9), custom_call_target="tpu_custom_call" | custom-call | tf_op jit(solution)/shard_map/pallas_call | solution.py:399
  98.5 1.0 copy.14
Async XLA Ops:
  59.7 2.2 %copy-start = (bf16[256,8192]{1,0:T(8,128)(2,1)S(1)}, bf16[256,8192]{1,0:T(8,128)(2,1)}, u32[]{:S(2)}) copy-start(bf16[256,8192]{1,0:T(8,128)(2,1)} %get-tuple-element.5.r_0_) | copy-start | bytes 12582916
